TPU v7x, 32 devices: a whole 2x2x4 slice. The times are simulated.
32 devices in a mesh: dp: 8 (over z, x), param: 4 (over y, core).
Axes of the slice: x: 2, y: 2, z: 4, core: 2. Of those that a mesh axis runs over, the one named last changes fastest.
Arguments:
- ex_grads: bfloat16 [768, 5120], P('dp', 'param'), may hold values from -6 to 6
- tgt_grads: bfloat16 [2048, 5120], P('dp', 'param'), may hold values from -6 to 6
- projection: bfloat16 [5120, 4096], P('param'), may hold values from -0.078125 to 0.078125
- example_weight: float32 [768], P('param'), may hold values from 0.05 to 1
Outputs:
- scores: float32 [2048, 768], P('dp', 'param')
All inputs are finite; a program needn't handle non-finite values.
Results may differ from a plain program's by a relative error of at most 0.0078.
Values may be sent and summed in bfloat16 or wider, within the bound.
A program may use at most 192 MiB of HBM per device.

v0:
```python
import math
import jax
import jax.numpy as jnp
from jax import lax
from jax.sharding import PartitionSpec as P

ridge_value = 0.5


def with_ridge(block, first_row):
    row_ids = lax.broadcasted_iota(jnp.int32, block.shape, 0) + first_row
    col_ids = lax.broadcasted_iota(jnp.int32, block.shape, 1)
    return block + jnp.where(row_ids == col_ids, ridge_value, 0.0).astype(jnp.float32)


def on_device(ex_grads, tgt_grads, projection, example_weight):
    ex_rows = ex_grads.shape[0]
    columns = projection.shape[1]
    param_total = lax.axis_size("param")
    param_pos = lax.axis_index("param")
    replica_pos = lax.axis_index("dp")
    stacked = jnp.concatenate([ex_grads, tgt_grads], axis=0)
    contract_rows = (((0,), (1,)), ((), ()))
    feature_block = lax.psum_scatter(
        lax.dot_general(projection, stacked, contract_rows, preferred_element_type=jnp.float32),
        "param",
        scatter_dimension=0,
        tiled=True,
    )
    local_features = feature_block.astype(jnp.bfloat16)
    example_part = local_features[:, :ex_rows]
    contract_first = (((0,), (0,)), ((), ()))
    partial_value = lax.dot_general(
        local_features,
        lax.all_gather(example_part, "dp", axis=1, tiled=True),
        contract_first,
        preferred_element_type=jnp.float32,
    )
    examples = partial_value.shape[1]
    summed = lax.psum(partial_value, "param")
    kernel_block = with_ridge(summed[:ex_rows] / columns, replica_pos * ex_rows)
    kernel = lax.all_gather(kernel_block, "dp", axis=0, tiled=True)
    cross_terms = summed[ex_rows:] / columns
    factor = jnp.linalg.cholesky(kernel)
    forward = jax.scipy.linalg.solve_triangular(factor, cross_terms.T, lower=True)
    solved = jax.scipy.linalg.solve_triangular(factor, forward, lower=True, trans=1)
    block_cols = examples // param_total
    chosen = lax.dynamic_slice_in_dim(solved.T, param_pos * block_cols, block_cols, 1)
    return chosen * math.sqrt(columns) * example_weight[None, :]


def solution(mesh):
    placed = (P("dp", "param"), P("dp", "param"), P("param", None), P("param"))
    return jax.shard_map(
        on_device, mesh=mesh, in_specs=placed, out_specs=P("dp", "param"), check_vma=False
    )
```

profile of v0, /device:TPU:0, one launch (start us, length us, event | category | flops | bytes accessed | tf_op | source)
XLA Modules:
  0.0 462.6 jit_solution(8862410163447170017)
XLA Ops:
  6.5 10.7 %convolution_bitcast_fusion = f32[4096,352]{0,1:T(8,128)} fusion(bf16[1280,4096]{1,0:T(8,128)(2,1)} %param.6, bf16[256,1280]{1,0:T(8,128)(2,1)} %param.5, bf16[96,1280]{1,0:T(8,128)(2,1)} %param.4), kind=kOutput, calls=%fused_computation.2 | convolution fusion | flops 3692789760 | bytes 17154048 | tf_op jit(solution)/shard_map/dot_general | solution.py:25
  17.3 57.3 %reduce-scatter.2.cloned.1.call-done = f32[1024,352]{0,1:T(8,128)} async-done(((f32[4096,352]{0,1:T(8,128)}), f32[1024,352]{0,1:T(8,128)}) %reduce-scatter.2.cloned.1.call-update) | async-done | bytes 1441808 | tf_op jit(solution)/shard_map/reduce_scatter | solution.py:24
  74.6 1.5 convert_element_type.3
  76.1 0.7 slice.254
  76.9 44.3 %all-gather.3.cloned.1.call-done = bf16[1024,768]{0,1:T(8,128)(2,1)} async-done(((bf16[1024,96]{0,1:T(8,128)(2,1)}), bf16[1024,768]{0,1:T(8,128)(2,1)}) %all-gather.3.cloned.1.call-update) | async-done | bytes 1572880 | tf_op jit(solution)/shard_map/all_gather | solution.py:35
  121.2 3.2 fusion.85
  124.4 35.1 %all-reduce.3.cloned.1.call-done = f32[352,768]{1,0:T(8,128)} async-done(((f32[352,768]{1,0:T(8,128)}), f32[352,768]{1,0:T(8,128)}) %all-reduce.3.cloned.1.call-update) | async-done | bytes 1081360 | tf_op jit(solution)/shard_map/psum | solution.py:40
  159.6 1.8 fusion.37
  161.4 0.6 iota_multiply_fusion
  162.0 1.2 fusion.4
  163.2 50.6 %all-gather.5.cloned.1.call-done = f32[768,768]{1,0:T(8,128)} async-done(((f32[96,768]{1,0:T(8,128)}), f32[768,768]{1,0:T(8,128)}) %all-gather.5.cloned.1.call-update) | async-done | bytes 2359312 | tf_op jit(solution)/shard_map/all_gather | solution.py:42
  213.8 3.3 copy.7
  217.1 2.0 fusion
  219.1 1.4 copy-done.2
  220.5 11.7 %cholesky.165 = f32[128,128]{1,0:T(8,128)S(1)} custom-call(f32[128,128]{1,0:T(8,128)S(1)} %cholesky.424), custom_call_target="Cholesky" | custom-call | tf_op jit(solution)/shard_map/jit(cholesky)/cholesky | solution.py:44
  232.4 9.8 %custom-call.50 = f32[1,128,128]{1,2,0:T(8,128)S(1)} custom-call(f32[1,128,128]{2,1,0:T(8,128)S(1)} %get-tuple-element.38), custom_call_target="InvertDiagBlocksLowerTriangular" | custom-call | tf_op jit(solution)/shard_map/jit(cholesky)/cholesky | solution.py:44
  242.2 1.4 constant_dynamic-update-slice_fusion.20
  243.6 1.4 convolution_subtract_fusion
  245.0 0.6 cholesky.428
  245.7 12.5 %cholesky.188 = f32[128,128]{1,0:T(8,128)S(1)} custom-call(f32[128,128]{1,0:T(8,128)} %cholesky.428), custom_call_target="Cholesky" | custom-call | tf_op jit(solution)/shard_map/jit(cholesky)/cholesky | solution.py:44
  258.2 0.6 select_reduce_fusion.4
  258.9 10.8 %custom-call.51 = f32[1,128,128]{1,2,0:T(8,128)S(1)} custom-call(f32[1,128,128]{2,1,0:T(8,128)} %get-tuple-element.35), custom_call_target="InvertDiagBlocksLowerTriangular" | custom-call | tf_op jit(solution)/shard_map/jit(cholesky)/cholesky | solution.py:44
  269.7 0.4 convolution_dynamic-update-slice_fusion
  270.1 1.5 convolution_subtract_fusion.1
  271.6 11.7 %cholesky.354 = f32[128,128]{1,0:T(8,128)S(1)} custom-call(f32[128,128]{1,0:T(8,128)S(1)} %cholesky.433), custom_call_target="Cholesky" | custom-call | tf_op jit(solution)/shard_map/jit(cholesky)/cholesky | solution.py:44
  283.4 9.8 %custom-call.52 = f32[1,128,128]{1,2,0:T(8,128)S(1)} custom-call(f32[1,128,128]{2,1,0:T(8,128)S(1)} %get-tuple-element.32), custom_call_target="InvertDiagBlocksLowerTriangular" | custom-call | tf_op jit(solution)/shard_map/jit(cholesky)/cholesky | solution.py:44
  293.5 1.6 convolution_subtract_fusion.2
  295.1 12.1 %cholesky.373 = f32[128,128]{1,0:T(8,128)S(1)} custom-call(f32[128,128]{1,0:T(8,128)S(1)} %cholesky.438), custom_call_target="Cholesky" | custom-call | tf_op jit(solution)/shard_map/jit(cholesky)/cholesky | solution.py:44
  307.3 9.8 %custom-call.53 = f32[1,128,128]{1,2,0:T(8,128)S(1)} custom-call(f32[1,128,128]{2,1,0:T(8,128)S(1)} %get-tuple-element.29), custom_call_target="InvertDiagBlocksLowerTriangular" | custom-call | tf_op jit(solution)/shard_map/jit(cholesky)/cholesky | solution.py:44
  317.4 1.5 convolution_subtract_fusion.11
  318.9 11.7 %cholesky.392 = f32[128,128]{1,0:T(8,128)S(1)} custom-call(f32[128,128]{1,0:T(8,128)S(1)} %cholesky.443), custom_call_target="Cholesky" | custom-call | tf_op jit(solution)/shard_map/jit(cholesky)/cholesky | solution.py:44
  330.6 9.8 %custom-call.54 = f32[1,128,128]{1,2,0:T(8,128)S(1)} custom-call(f32[1,128,128]{2,1,0:T(8,128)S(1)} %get-tuple-element.26), custom_call_target="InvertDiagBlocksLowerTriangular" | custom-call | tf_op jit(solution)/shard_map/jit(cholesky)/cholesky | solution.py:44
  340.6 1.3 convolution_subtract_fusion.14
  342.0 11.9 %cholesky.410 = f32[128,128]{1,0:T(8,128)S(1)} custom-call(f32[128,128]{1,0:T(8,128)S(1)} %convolution_subtract_fusion.14), custom_call_target="Cholesky" | custom-call | tf_op jit(solution)/shard_map/jit(cholesky)/cholesky | solution.py:44
  353.9 0.7 compare_reduce_fusion.3
  354.6 0.6 compare_reduce_fusion.2
  355.2 0.7 compare_reduce_fusion.1
  355.9 0.7 compare_reduce_fusion
  356.6 0.7 compare_reduce_fusion.4
  361.0 1.6 select_select_fusion
  362.6 20.5 %while.1 = (s32[]{:T(128)}, f32[768,768]{1,0:T(8,128)}, s32[6,2]{0,1:T(2,128)S(1)}, f32[6,128,128]{2,1,0:T(8,128)}, s32[]{:T(128)}) while((s32[]{:T(128)}, f32[768,768]{1,0:T(8,128)}, s32[6,2]{0,1:T(2,128)S(1)}, f32[6,128,128]{2,1,0:T(8,128)}, s32[]{:T(128)}) %tuple.37), condition=%wide.while_cond, body=%wide.while_body.sunk | while | flops 2 | bytes 132205 | solution.py:46
  362.7 0.5 fusion.106
  363.2 2.8 bitcast_dynamic-update-slice_fusion.2
  366.1 0.5 fusion.106
  366.6 2.8 bitcast_dynamic-update-slice_fusion.2
  369.5 0.5 fusion.106
  370.1 2.8 bitcast_dynamic-update-slice_fusion.2
  372.9 0.5 fusion.106
  373.5 2.8 bitcast_dynamic-update-slice_fusion.2
  376.4 0.5 fusion.106
  376.9 2.8 bitcast_dynamic-update-slice_fusion.2
  379.8 0.5 fusion.106
  380.3 2.8 bitcast_dynamic-update-slice_fusion.2
  383.1 59.9 %custom-call.55 = f32[6,128,128]{1,2,0:T(8,128)S(1)} custom-call(f32[6,128,128]{2,1,0:T(8,128)} %get-tuple-element.12), custom_call_target="InvertDiagBlocksLowerTriangular" | custom-call | tf_op jit(solution)/shard_map/jit(_solve_triangular)/triangular_solve | solution.py:46
  443.3 1.2 convolution_subtract_fusion.13
  444.9 1.5 convolution_subtract_fusion.10
  446.7 0.8 convolution_subtract_fusion.9
  447.8 1.0 convolution_subtract_fusion.8
  449.2 1.3 convolution_subtract_fusion.7
  451.6 0.4 convolution_subtract_fusion.6
  452.3 0.5 convolution_subtract_fusion.5
  453.1 0.6 convolution_subtract_fusion.4
  454.0 0.7 convolution_subtract_fusion.3
  455.1 0.8 multiply_bitcast_fusion
  (62 shorter events, 5.6 us)
Async XLA Ops:
  6.5 68.1 %reduce-scatter.2.cloned.1.call-start = ((), (), s32[]{:S(2)}) async-start(), calls=%async_computation.1 | async-start | bytes 7208960 | tf_op jit(solution)/shard_map/reduce_scatter | solution.py:24
  17.2 103.9 %all-gather.3.cloned.1.call-start = ((), (), s32[]{:S(2)}) async-start(), calls=%async_computation.2 | async-start | bytes 1769472 | tf_op jit(solution)/shard_map/all_gather | solution.py:35
  76.8 85.2 %copy-start.3 = (f32[192]{0:T(256)S(1)}, f32[192]{0:T(256)}, u32[]{:S(2)}) copy-start(f32[192]{0:T(256)} %param.7) | copy-start | bytes 2308
  76.8 82.7 %all-reduce.3.cloned.1.call-start = ((), (), s32[]{:S(2)}) async-start(), calls=%async_computation.3 | async-start | bytes 2162688 | tf_op jit(solution)/shard_map/psum | solution.py:40
  124.4 89.4 %all-gather.5.cloned.1.call-start = ((), (), s32[]{:S(2)}) async-start(), calls=%async_computation.4 | async-start | bytes 2654208 | tf_op jit(solution)/shard_map/all_gather | solution.py:42
  213.8 3.3 copy-start
  219.1 1.4 copy-start.2
  361.0 1.6 copy-start.4
  383.1 63.6 %copy-start.1 = (f32[768,768]{1,0:T(8,128)S(1)}, f32[768,768]{1,0:T(8,128)}, u32[]{:S(2)}) copy-start(f32[768,768]{1,0:T(8,128)} %get-tuple-element.104) | copy-start | bytes 7077892
Sparse Core Ops, SparseCore 0:
  17.4 57.2 reduce-scatter.1
  77.0 44.1 all-gather.2
  124.5 35.0 all-reduce.2
  161.6 52.1 all-gather.4
where the time goes:
time: 467 us; the launch traced here: 463 us
  other arithmetic  195 us (42%)
  waiting for transfers between devices  187 us (40%)
  matrix products  35.5 us (8%)
  local copies, waits for them, and re-layouts  26.8 us (6%)
  between operations  17.6 us (4%)
    another operation x22, other arithmetic, on_device(): factor = jnp.linalg.cholesky(kernel)  126 us
    another operation x3, other arithmetic, on_device(): jax.scipy.linalg.solve_triangular(factor, forward, lower=True, trans=1)  62.1 us
    reduce_scatter x1, waiting for transfers between devices, on_device(): lax.psum_scatter(lax.dot_general(projection, stacked, contract_rows, pref...  57.3 us
    all_gather x1, waiting for transfers between devices, on_device(): kernel = lax.all_gather(kernel_block, 'dp', axis=0, tiled=True)  50.6 us
    all_gather x1, waiting for transfers between devices, on_device(): lax.all_gather(example_part, 'dp', axis=1, tiled=True)  44.3 us
    psum x1, waiting for transfers between devices, on_device(): summed = lax.psum(partial_value, 'param')  35.1 us
    another operation x18, local copies, waits for them, and re-layouts  20.4 us
    dot_general x1, matrix products, on_device(): lax.dot_general(projection, stacked, contract_rows, preferred_element_typ...  10.7 us
  transfers between devices with their start and end apart: 4, of which 4 were waited for; matrix products, arithmetic and copies ran while one was open for 0% of the time, Pallas kernels for 0%

commit v1 on v0

--- a/solution.py
+++ b/solution.py
@@ -37,7 +37,22 @@
         preferred_element_type=jnp.float32,
     )
     examples = partial_value.shape[1]
-    summed = lax.psum(partial_value, "param")
+
+    def plan_masks(field_in, along_axis):
+        workers = lax.axis_size(along_axis)
+
+        def bind_types(local_now, r_now):
+            if r_now >= workers:
+                return local_now
+            y1 = tuple(((dev_j, dev_j ^ r_now) for dev_j in range(workers)))
+            b_now = lax.ppermute(local_now, along_axis, y1)
+            then = bind_types(local_now + b_now, 2 * r_now)
+            return then
+
+        out_arr = bind_types(field_in, 1)
+        return out_arr
+
+    summed = plan_masks(partial_value, "param")
     kernel_block = with_ridge(summed[:ex_rows] / columns, replica_pos * ex_rows)
     kernel = lax.all_gather(kernel_block, "dp", axis=0, tiled=True)
     cross_terms = summed[ex_rows:] / columns

time: 467 us -> 457 us (0.979)
  waiting for transfers between devices: 187 us -> 178 us
    psum x1 -> x0, waiting for transfers between devices: 35.1 us -> none  [on_device(): summed = lax.psum(partial_value, 'param')]
    ppermute x0 -> x2, waiting for transfers between devices: none -> 27.1 us  [bind_types(): b_now = lax.ppermute(local_now, along_axis, y1)]
  transfers between devices with their start and end apart: 4 -> 5, of which waited for: 4 -> 5; matrix products, arithmetic and copies ran while one was open for 0% -> 0% of each run, Pallas kernels for 0% -> 0%
where the time goes in v1:
time: 457 us; the launch traced here: 452 us
  other arithmetic  193 us (42%)
  waiting for transfers between devices  178 us (39%)
  matrix products  34.5 us (8%)
  local copies, waits for them, and re-layouts  26.8 us (6%)
  between operations  17.6 us (4%)
    another operation x22, other arithmetic, on_device(): factor = jnp.linalg.cholesky(kernel)  126 us
    another operation x3, other arithmetic, on_device(): jax.scipy.linalg.solve_triangular(factor, forward, lower=True, trans=1)  62.1 us
    reduce_scatter x1, waiting for transfers between devices, on_device(): lax.psum_scatter(lax.dot_general(projection, stacked, contract_rows, pref...  57.3 us
    all_gather x1, waiting for transfers between devices, on_device(): kernel = lax.all_gather(kernel_block, 'dp', axis=0, tiled=True)  49.7 us
    all_gather x1, waiting for transfers between devices, on_device(): lax.all_gather(example_part, 'dp', axis=1, tiled=True)  44.3 us
    ppermute x2, waiting for transfers between devices, bind_types(): b_now = lax.ppermute(local_now, along_axis, y1)  27.1 us
    another operation x18, local copies, waits for them, and re-layouts  20.4 us
    dot_general x1, matrix products, on_device(): lax.dot_general(projection, stacked, contract_rows, preferred_element_typ...  10.7 us
  transfers between devices with their start and end apart: 5, of which 5 were waited for; matrix products, arithmetic and copies ran while one was open for 0% of the time, Pallas kernels for 0%

profile of v1, /device:TPU:0, one launch (start us, length us, event | category | flops | bytes accessed | tf_op | source)
XLA Modules:
  0.0 452.4 jit_solution(6952331860185271510)
XLA Ops:
  6.5 10.7 %convolution_bitcast_fusion = f32[4096,352]{0,1:T(8,128)} fusion(bf16[1280,4096]{1,0:T(8,128)(2,1)} %param.6, bf16[256,1280]{1,0:T(8,128)(2,1)} %param.5, bf16[96,1280]{1,0:T(8,128)(2,1)} %param.4), kind=kOutput, calls=%fused_computation.2 | convolution fusion | flops 3692789760 | bytes 17154048 | tf_op jit(solution)/shard_map/dot_general | solution.py:25
  17.3 57.3 %reduce-scatter.2.cloned.1.call-done = f32[1024,352]{0,1:T(8,128)} async-done(((f32[4096,352]{0,1:T(8,128)}), f32[1024,352]{0,1:T(8,128)}) %reduce-scatter.2.cloned.1.call-update) | async-done | bytes 1441808 | tf_op jit(solution)/shard_map/reduce_scatter | solution.py:24
  74.6 1.5 convert_element_type.3
  76.1 0.7 slice.254
  76.9 44.3 %all-gather.3.cloned.1.call-done = bf16[1024,768]{0,1:T(8,128)(2,1)} async-done(((bf16[1024,96]{0,1:T(8,128)(2,1)}), bf16[1024,768]{0,1:T(8,128)(2,1)}) %all-gather.3.cloned.1.call-update) | async-done | bytes 1572880 | tf_op jit(solution)/shard_map/all_gather | solution.py:35
  121.2 2.2 fusion.90
  123.4 2.7 collective-permute-done
  126.3 1.5 collective-permute-start.1
  127.8 24.4 %collective-permute-done.1 = f32[352,768]{1,0:T(8,128)S(1)} collective-permute-done((f32[352,768]{1,0:T(8,128)S(1)}, f32[352,768]{1,0:T(8,128)S(1)}, u32[]{:S(2)}, u32[]{:S(2)}) %collective-permute-start.1) | collective-permute-done | bytes 1081376 | tf_op jit(solution)/shard_map/ppermute | solution.py:48
  152.4 0.8 fusion.40
  153.2 0.6 iota_multiply_fusion
  153.9 49.7 %all-gather.5.cloned.1.call-done = f32[768,768]{1,0:T(8,128)} async-done(((f32[96,768]{1,0:T(8,128)}), f32[768,768]{1,0:T(8,128)}) %all-gather.5.cloned.1.call-update) | async-done | bytes 2359312 | tf_op jit(solution)/shard_map/all_gather | solution.py:57
  203.5 3.3 copy.8
  206.9 2.0 fusion
  208.9 1.4 copy-done.2
  210.3 11.7 %cholesky.165 = f32[128,128]{1,0:T(8,128)S(1)} custom-call(f32[128,128]{1,0:T(8,128)S(1)} %cholesky.424), custom_call_target="Cholesky" | custom-call | tf_op jit(solution)/shard_map/jit(cholesky)/cholesky | solution.py:59
  222.2 9.8 %custom-call.50 = f32[1,128,128]{1,2,0:T(8,128)S(1)} custom-call(f32[1,128,128]{2,1,0:T(8,128)S(1)} %get-tuple-element.38), custom_call_target="InvertDiagBlocksLowerTriangular" | custom-call | tf_op jit(solution)/shard_map/jit(cholesky)/cholesky | solution.py:59
  232.0 1.4 constant_dynamic-update-slice_fusion.20
  233.4 1.4 convolution_subtract_fusion
  234.8 0.6 cholesky.428
  235.4 12.5 %cholesky.188 = f32[128,128]{1,0:T(8,128)S(1)} custom-call(f32[128,128]{1,0:T(8,128)} %cholesky.428), custom_call_target="Cholesky" | custom-call | tf_op jit(solution)/shard_map/jit(cholesky)/cholesky | solution.py:59
  248.0 0.6 select_reduce_fusion.4
  248.6 10.8 %custom-call.51 = f32[1,128,128]{1,2,0:T(8,128)S(1)} custom-call(f32[1,128,128]{2,1,0:T(8,128)} %get-tuple-element.35), custom_call_target="InvertDiagBlocksLowerTriangular" | custom-call | tf_op jit(solution)/shard_map/jit(cholesky)/cholesky | solution.py:59
  259.8 1.5 convolution_subtract_fusion.1
  261.4 11.7 %cholesky.354 = f32[128,128]{1,0:T(8,128)S(1)} custom-call(f32[128,128]{1,0:T(8,128)S(1)} %cholesky.433), custom_call_target="Cholesky" | custom-call | tf_op jit(solution)/shard_map/jit(cholesky)/cholesky | solution.py:59
  273.1 9.8 %custom-call.52 = f32[1,128,128]{1,2,0:T(8,128)S(1)} custom-call(f32[1,128,128]{2,1,0:T(8,128)S(1)} %get-tuple-element.32), custom_call_target="InvertDiagBlocksLowerTriangular" | custom-call | tf_op jit(solution)/shard_map/jit(cholesky)/cholesky | solution.py:59
  283.3 1.6 convolution_subtract_fusion.2
  284.9 12.1 %cholesky.373 = f32[128,128]{1,0:T(8,128)S(1)} custom-call(f32[128,128]{1,0:T(8,128)S(1)} %cholesky.438), custom_call_target="Cholesky" | custom-call | tf_op jit(solution)/shard_map/jit(cholesky)/cholesky | solution.py:59
  297.0 9.8 %custom-call.53 = f32[1,128,128]{1,2,0:T(8,128)S(1)} custom-call(f32[1,128,128]{2,1,0:T(8,128)S(1)} %get-tuple-element.29), custom_call_target="InvertDiagBlocksLowerTriangular" | custom-call | tf_op jit(solution)/shard_map/jit(cholesky)/cholesky | solution.py:59
  307.1 1.5 convolution_subtract_fusion.7
  308.6 11.7 %cholesky.392 = f32[128,128]{1,0:T(8,128)S(1)} custom-call(f32[128,128]{1,0:T(8,128)S(1)} %cholesky.443), custom_call_target="Cholesky" | custom-call | tf_op jit(solution)/shard_map/jit(cholesky)/cholesky | solution.py:59
  320.4 9.8 %custom-call.54 = f32[1,128,128]{1,2,0:T(8,128)S(1)} custom-call(f32[1,128,128]{2,1,0:T(8,128)S(1)} %get-tuple-element.26), custom_call_target="InvertDiagBlocksLowerTriangular" | custom-call | tf_op jit(solution)/shard_map/jit(cholesky)/cholesky | solution.py:59
  330.4 1.3 convolution_subtract_fusion.9
  331.7 11.9 %cholesky.410 = f32[128,128]{1,0:T(8,128)S(1)} custom-call(f32[128,128]{1,0:T(8,128)S(1)} %convolution_subtract_fusion.9), custom_call_target="Cholesky" | custom-call | tf_op jit(solution)/shard_map/jit(cholesky)/cholesky | solution.py:59
  343.6 0.7 compare_reduce_fusion.3
  344.3 0.6 compare_reduce_fusion.2
  345.0 0.7 compare_reduce_fusion.1
  345.6 0.7 compare_reduce_fusion
  346.3 0.7 compare_reduce_fusion.4
  350.8 1.6 select_select_fusion
  352.4 20.5 %while.1 = (s32[]{:T(128)}, f32[768,768]{1,0:T(8,128)}, s32[6,2]{0,1:T(2,128)S(1)}, f32[6,128,128]{2,1,0:T(8,128)}, s32[]{:T(128)}) while((s32[]{:T(128)}, f32[768,768]{1,0:T(8,128)}, s32[6,2]{0,1:T(2,128)S(1)}, f32[6,128,128]{2,1,0:T(8,128)}, s32[]{:T(128)}) %tuple.37), condition=%wide.while_cond, body=%wide.while_body.sunk | while | flops 2 | bytes 132205 | solution.py:61
  352.4 0.5 fusion.106
  353.0 2.8 bitcast_dynamic-update-slice_fusion.2
  355.9 0.5 fusion.106
  356.4 2.8 bitcast_dynamic-update-slice_fusion.2
  359.3 0.5 fusion.106
  359.8 2.8 bitcast_dynamic-update-slice_fusion.2
  362.7 0.5 fusion.106
  363.2 2.8 bitcast_dynamic-update-slice_fusion.2
  366.1 0.5 fusion.106
  366.7 2.8 bitcast_dynamic-update-slice_fusion.2
  369.5 0.5 fusion.106
  370.1 2.8 bitcast_dynamic-update-slice_fusion.2
  372.8 59.9 %custom-call.55 = f32[6,128,128]{1,2,0:T(8,128)S(1)} custom-call(f32[6,128,128]{2,1,0:T(8,128)} %get-tuple-element.12), custom_call_target="InvertDiagBlocksLowerTriangular" | custom-call | tf_op jit(solution)/shard_map/jit(_solve_triangular)/triangular_solve | solution.py:61
  433.1 1.2 fusion.68
  434.6 1.5 fusion.45
  436.5 0.8 fusion.23
  437.6 1.0 fusion.8
  438.9 1.3 fusion.34
  441.4 0.4 convolution_subtract_fusion.6
  442.1 0.5 convolution_subtract_fusion.5
  442.8 0.6 convolution_subtract_fusion.4
  443.8 0.7 convolution_subtract_fusion.3
  444.9 0.8 multiply_bitcast_fusion
  (65 shorter events, 6.3 us)
Async XLA Ops:
  6.5 68.1 %reduce-scatter.2.cloned.1.call-start = ((), (), s32[]{:S(2)}) async-start(), calls=%async_computation.1 | async-start | bytes 7208960 | tf_op jit(solution)/shard_map/reduce_scatter | solution.py:24
  17.2 103.9 %all-gather.3.cloned.1.call-start = ((), (), s32[]{:S(2)}) async-start(), calls=%async_computation.2 | async-start | bytes 1769472 | tf_op jit(solution)/shard_map/all_gather | solution.py:35
  76.8 126.7 %all-gather.5.cloned.1.call-start = ((), (), s32[]{:S(2)}) async-start(), calls=%async_computation.3 | async-start | bytes 2654208 | tf_op jit(solution)/shard_map/all_gather | solution.py:57
  123.3 2.8 collective-permute-start
  126.2 27.6 %copy-start.3 = (f32[192]{0:T(256)S(1)}, f32[192]{0:T(256)}, u32[]{:S(2)}) copy-start(f32[192]{0:T(256)} %param.7) | copy-start | bytes 2308
  126.3 26.0 %collective-permute-start.1 = (f32[352,768]{1,0:T(8,128)S(1)}, f32[352,768]{1,0:T(8,128)S(1)}, u32[]{:S(2)}, u32[]{:S(2)}) collective-permute-start(f32[352,768]{1,0:T(8,128)S(1)} %add.83), channel_id=1, source_target_pairs={{0,2},{1,3},{2,0},{3,1},{4,6},{5,7},{6,4},{7,5},{8,10},{9,11},{10,... | collective-permute-start | bytes 3244040 | tf_op jit(solution)/shard_map/ppermute | solution.py:48
  203.5 3.3 copy-start
  208.9 1.4 copy-start.2
  350.8 1.6 copy-start.4
  372.8 63.6 %copy-start.1 = (f32[768,768]{1,0:T(8,128)S(1)}, f32[768,768]{1,0:T(8,128)}, u32[]{:S(2)}) copy-start(f32[768,768]{1,0:T(8,128)} %get-tuple-element.103) | copy-start | bytes 7077892
Sparse Core Ops, SparseCore 0:
  17.4 57.2 reduce-scatter.1
  77.0 44.1 all-gather.2
  153.3 50.1 all-gather.4
